TPU v7x, 32 devices: a whole 2x2x4 slice. The times are simulated.
32 devices in a mesh: sky: 4 (over x, core), tm: 8 (over z, y).
Axes of the slice: x: 2, y: 2, z: 4, core: 2. Of those that a mesh axis runs over, the one named last changes fastest.
Arguments:
- attitude: float32 [4, 8, 512], P(None, 'tm', 'sky'), may hold values from -6 to 6
- slot_time: float32 [262144], P(('sky', 'tm')), may hold values from -1 to 1
- slot_parallax: float32 [262144], P(('sky', 'tm')), may hold values from -1 to 1
- slot_observed: float32 [262144], P(('sky', 'tm')), may hold values from -6 to 6
- slot_phase: float32 [262144], P(('sky', 'tm')), may hold values from 0 to 1
- slot_knot: int32 [262144], P(('sky', 'tm')), may hold values from 0 to 508
- block_source: int32 [8192], P(('sky', 'tm')), may hold values from 0 to 63
- block_count: int32 [8192], P(('sky', 'tm')), may hold values from 1 to 32
- prior: float32 [5, 256], P(None, ('sky', 'tm')), may hold values from 0.5 to 4
Outputs:
- update: float32 [5, 256], P(None, ('sky', 'tm'))
Inputs may be any that keep to these rules, and one draw needn't show every extreme that they name: The four knots from slot_knot on lie in the transit's time group of 512 knots. `block_source`: an index into the 64 sources of the block's own sky sector.
All inputs are finite; a program needn't handle non-finite values.
Results may differ from a plain program's by a relative error of at most 0.0003.
Values sent between devices are 32-bit elements; how exact they have to be, the bound alone decides.
A program may use at most 64 MiB of HBM per device.

v0:
```python
import math
import jax
import jax.numpy as jnp
from jax import lax
from jax.sharding import PartitionSpec as P

PAIR_LIST = [(i, j) for i in range(5) for j in range(i, 5)]


def spline_quat(table, knot, phase):
    total = knot.shape[0]
    width = table.shape[1]
    step = math.gcd(total, 512)
    knot_rows = knot.reshape(total // step, step)
    phase_rows = phase.reshape(total // step, step)
    positions = jnp.arange(width, dtype=jnp.int32)

    def one_block(items):
        knot_here, phase_here = items
        weights = [
            (1.0 - phase_here) ** 3 / 6.0,
            (3.0 * phase_here**3 - 6.0 * phase_here**2 + 4.0) / 6.0,
            (-3.0 * phase_here**3 + 3.0 * phase_here**2 + 3.0 * phase_here + 1.0) / 6.0,
            phase_here**3 / 6.0,
        ]
        offset = positions[None, :] - knot_here[:, None]
        spread = jnp.zeros((step, width), jnp.float32)
        for i in range(4):
            spread = jnp.where(offset == i, weights[i][:, None], spread)
        return lax.dot_general(
            table,
            spread,
            (((1,), (1,)), ((), ())),
            precision=lax.Precision.HIGHEST,
            preferred_element_type=jnp.float32,
        )

    quat = lax.map(one_block, (knot_rows, phase_rows))
    return jnp.transpose(quat, (1, 0, 2)).reshape(4, total)


def block_sums(table, knot, phase, time, parallax, observed, count):
    quat = spline_quat(table, knot, phase)
    cross = quat[0] * quat[0] + quat[1] * quat[1] - quat[2] * quat[2] - quat[3] * quat[3]
    along = 2.0 * (quat[1] * quat[2] + quat[0] * quat[3])
    tilt = 2.0 * (quat[1] * quat[3] - quat[0] * quat[2])
    design = [cross, along, parallax, time * cross, time * along]
    residual = observed - tilt
    rows = [design[i] * design[j] for i, j in PAIR_LIST] + [design[i] * residual for i in range(5)]
    stacked = jnp.stack(rows)
    blocks = count.shape[0]
    stacked = stacked.reshape(20, blocks, -1)
    live = (jnp.arange(stacked.shape[2], dtype=jnp.int32)[None, :] < count[:, None]).astype(
        stacked.dtype
    )
    return jnp.sum(stacked * live[None], axis=2)


def source_sums(sums, block_source, sector_sources):
    blocks = block_source.shape[0]
    step = math.gcd(blocks, 512)
    source_rows = block_source.reshape(blocks // step, step)
    sum_rows = jnp.transpose(sums.reshape(20, blocks // step, step), (1, 0, 2))
    positions = jnp.arange(sector_sources, dtype=jnp.int32)

    def add_block(carry, items):
        source_here, sums_here = items
        member = (source_here[:, None] == positions[None, :]).astype(jnp.float32)
        return (
            carry
            + jnp.dot(
                sums_here,
                member,
                precision=lax.Precision.HIGHEST,
                preferred_element_type=jnp.float32,
            ),
            None,
        )

    start = jnp.zeros((20, sector_sources), jnp.float32)
    total, _ = lax.scan(add_block, start, (source_rows, sum_rows))
    return total


def solve_normals(normal, prior):
    entry = {}
    for index, pair in enumerate(PAIR_LIST):
        entry[pair[1], pair[0]] = normal[index]
    for i in range(5):
        entry[i, i] = entry[i, i] + prior[i]
    lower = {}
    for col in range(5):
        pivot = entry[col, col]
        for k in range(col):
            pivot = pivot - lower[col, k] * lower[col, k]
        root = jnp.sqrt(pivot)
        lower[col, col] = root
        for row in range(col + 1, 5):
            value = entry[row, col]
            for k in range(col):
                value = value - lower[row, k] * lower[col, k]
            lower[row, col] = value / root
    forward = []
    for i in range(5):
        value = normal[15 + i]
        for k in range(i):
            value = value - lower[i, k] * forward[k]
        forward.append(value / lower[i, i])
    result = [None] * 5
    for i in range(4, -1, -1):
        value = forward[i]
        for k in range(i + 1, 5):
            value = value - lower[k, i] * result[k]
        result[i] = value / lower[i, i]
    return jnp.stack(result)


def on_device(
    attitude,
    slot_time,
    slot_parallax,
    slot_observed,
    slot_phase,
    slot_knot,
    block_source,
    block_count,
    prior,
):
    group = lax.all_gather(attitude, "sky", axis=2, tiled=True)
    table = group[:, 0, :]
    sums = block_sums(
        table, slot_knot, slot_phase, slot_time, slot_parallax, slot_observed, block_count
    )
    owned = prior.shape[1]
    sector_sources = owned * lax.axis_size("tm")
    partial_value = source_sums(sums, block_source, sector_sources)
    total = lax.psum(partial_value, "tm")
    normal = lax.dynamic_slice_in_dim(total, lax.axis_index("tm") * owned, owned, 1)
    return solve_normals(normal, prior)


def solution(mesh):
    in_specs = (
        P(None, "tm", "sky"),
        P(("sky", "tm")),
        P(("sky", "tm")),
        P(("sky", "tm")),
        P(("sky", "tm")),
        P(("sky", "tm")),
        P(("sky", "tm")),
        P(("sky", "tm")),
        P(None, ("sky", "tm")),
    )
    out_specs = P(None, ("sky", "tm"))
    return jax.shard_map(
        on_device, mesh=mesh, in_specs=in_specs, out_specs=out_specs, check_vma=False
    )
```

profile of v0, /device:TPU:0, one launch (start us, length us, event | category | flops | bytes accessed | tf_op | source)
XLA Modules:
  0.0 77.9 jit_solution(18191354367063263991)
XLA Ops:
  0.0 0.8 reshape.292
  0.8 0.7 copy-done.4
  1.5 6.2 %all_gather.3 = f32[4,1,512]{2,0,1:T(4,128)S(1)} all-gather(f32[4,1,128]{2,0,1:T(4,128)S(1)} %bitcast.33), channel_id=1, replica_groups=mesh['sky'=4,'tm'=8] {'sky'}, dimensions={2}, use_global_device_ids=true | all-gather | bytes 10240 | tf_op jit(solution)/shard_map/all_gather | solution.py:129
  7.6 22.9 %while.3 = (s32[]{:T(128)}, f32[16,4,512]{2,1,0:T(4,128)S(1)}, s32[16,512]{1,0:T(8,128)S(1)}, f32[16,512]{1,0:T(8,128)S(1)}, f32[4,512]{1,0:T(4,128)S(1)}, /*index=5*/s32[]{:T(128)}) while((s32[]{:T(128)}, f32[16,4,512]{2,1,0:T(4,128)S(1)}, s32[16,512]{1,0:T(8,128)S(1)}, f32[16,512]{1,0:T(8,128)S(1)}, f32[4,512]{1,0:T(4,128)S(1)}, ...), condition=%wide.region_1.2_spmd.clone, body=%wide.region_0.1_spmd.clone.sunk | while | flops 14951938 | bytes 45145 | solution.py:38
  7.6 1.4 %fusion.59 = f32[16,4,512]{2,1,0:T(4,128)S(1)} fusion(f32[16,4,512]{2,1,0:T(4,128)S(1)} %get-tuple-element.192, s32[]{:T(128)S(6)} %copy.59, f32[4,512]{1,0:T(4,128)S(1)} %get-tuple-element.201, f32[512]{0:T(512)S(1)} %get-tuple-element.181, f32[512]{0:T(512)S(1)} %get-tuple-element.182, f32[512]{0:T(512)S(1)} %get-tuple-element.183, ...), kind=kOutput, calls=%fused_computation.2.clone.1 | convolution fusion | flops 14942208 | bytes 26628 | tf_op jit(solution)/shard_map/while/body/eval_jaxpr/dot_general | solution.py:30
  9.1 1.4 %fusion.59 = f32[16,4,512]{2,1,0:T(4,128)S(1)} fusion(f32[16,4,512]{2,1,0:T(4,128)S(1)} %get-tuple-element.192, s32[]{:T(128)S(6)} %copy.59, f32[4,512]{1,0:T(4,128)S(1)} %get-tuple-element.201, f32[512]{0:T(512)S(1)} %get-tuple-element.181, f32[512]{0:T(512)S(1)} %get-tuple-element.182, f32[512]{0:T(512)S(1)} %get-tuple-element.183, ...), kind=kOutput, calls=%fused_computation.2.clone.1 | convolution fusion | flops 14942208 | bytes 26628 | tf_op jit(solution)/shard_map/while/body/eval_jaxpr/dot_general | solution.py:30
  10.5 1.4 %fusion.59 = f32[16,4,512]{2,1,0:T(4,128)S(1)} fusion(f32[16,4,512]{2,1,0:T(4,128)S(1)} %get-tuple-element.192, s32[]{:T(128)S(6)} %copy.59, f32[4,512]{1,0:T(4,128)S(1)} %get-tuple-element.201, f32[512]{0:T(512)S(1)} %get-tuple-element.181, f32[512]{0:T(512)S(1)} %get-tuple-element.182, f32[512]{0:T(512)S(1)} %get-tuple-element.183, ...), kind=kOutput, calls=%fused_computation.2.clone.1 | convolution fusion | flops 14942208 | bytes 26628 | tf_op jit(solution)/shard_map/while/body/eval_jaxpr/dot_general | solution.py:30
  12.0 1.4 %fusion.59 = f32[16,4,512]{2,1,0:T(4,128)S(1)} fusion(f32[16,4,512]{2,1,0:T(4,128)S(1)} %get-tuple-element.192, s32[]{:T(128)S(6)} %copy.59, f32[4,512]{1,0:T(4,128)S(1)} %get-tuple-element.201, f32[512]{0:T(512)S(1)} %get-tuple-element.181, f32[512]{0:T(512)S(1)} %get-tuple-element.182, f32[512]{0:T(512)S(1)} %get-tuple-element.183, ...), kind=kOutput, calls=%fused_computation.2.clone.1 | convolution fusion | flops 14942208 | bytes 26628 | tf_op jit(solution)/shard_map/while/body/eval_jaxpr/dot_general | solution.py:30
  13.4 1.4 %fusion.59 = f32[16,4,512]{2,1,0:T(4,128)S(1)} fusion(f32[16,4,512]{2,1,0:T(4,128)S(1)} %get-tuple-element.192, s32[]{:T(128)S(6)} %copy.59, f32[4,512]{1,0:T(4,128)S(1)} %get-tuple-element.201, f32[512]{0:T(512)S(1)} %get-tuple-element.181, f32[512]{0:T(512)S(1)} %get-tuple-element.182, f32[512]{0:T(512)S(1)} %get-tuple-element.183, ...), kind=kOutput, calls=%fused_computation.2.clone.1 | convolution fusion | flops 14942208 | bytes 26628 | tf_op jit(solution)/shard_map/while/body/eval_jaxpr/dot_general | solution.py:30
  14.8 1.4 %fusion.59 = f32[16,4,512]{2,1,0:T(4,128)S(1)} fusion(f32[16,4,512]{2,1,0:T(4,128)S(1)} %get-tuple-element.192, s32[]{:T(128)S(6)} %copy.59, f32[4,512]{1,0:T(4,128)S(1)} %get-tuple-element.201, f32[512]{0:T(512)S(1)} %get-tuple-element.181, f32[512]{0:T(512)S(1)} %get-tuple-element.182, f32[512]{0:T(512)S(1)} %get-tuple-element.183, ...), kind=kOutput, calls=%fused_computation.2.clone.1 | convolution fusion | flops 14942208 | bytes 26628 | tf_op jit(solution)/shard_map/while/body/eval_jaxpr/dot_general | solution.py:30
  16.3 1.4 %fusion.59 = f32[16,4,512]{2,1,0:T(4,128)S(1)} fusion(f32[16,4,512]{2,1,0:T(4,128)S(1)} %get-tuple-element.192, s32[]{:T(128)S(6)} %copy.59, f32[4,512]{1,0:T(4,128)S(1)} %get-tuple-element.201, f32[512]{0:T(512)S(1)} %get-tuple-element.181, f32[512]{0:T(512)S(1)} %get-tuple-element.182, f32[512]{0:T(512)S(1)} %get-tuple-element.183, ...), kind=kOutput, calls=%fused_computation.2.clone.1 | convolution fusion | flops 14942208 | bytes 26628 | tf_op jit(solution)/shard_map/while/body/eval_jaxpr/dot_general | solution.py:30
  17.7 1.4 %fusion.59 = f32[16,4,512]{2,1,0:T(4,128)S(1)} fusion(f32[16,4,512]{2,1,0:T(4,128)S(1)} %get-tuple-element.192, s32[]{:T(128)S(6)} %copy.59, f32[4,512]{1,0:T(4,128)S(1)} %get-tuple-element.201, f32[512]{0:T(512)S(1)} %get-tuple-element.181, f32[512]{0:T(512)S(1)} %get-tuple-element.182, f32[512]{0:T(512)S(1)} %get-tuple-element.183, ...), kind=kOutput, calls=%fused_computation.2.clone.1 | convolution fusion | flops 14942208 | bytes 26628 | tf_op jit(solution)/shard_map/while/body/eval_jaxpr/dot_general | solution.py:30
  19.1 1.4 %fusion.59 = f32[16,4,512]{2,1,0:T(4,128)S(1)} fusion(f32[16,4,512]{2,1,0:T(4,128)S(1)} %get-tuple-element.192, s32[]{:T(128)S(6)} %copy.59, f32[4,512]{1,0:T(4,128)S(1)} %get-tuple-element.201, f32[512]{0:T(512)S(1)} %get-tuple-element.181, f32[512]{0:T(512)S(1)} %get-tuple-element.182, f32[512]{0:T(512)S(1)} %get-tuple-element.183, ...), kind=kOutput, calls=%fused_computation.2.clone.1 | convolution fusion | flops 14942208 | bytes 26628 | tf_op jit(solution)/shard_map/while/body/eval_jaxpr/dot_general | solution.py:30
  20.6 1.4 %fusion.59 = f32[16,4,512]{2,1,0:T(4,128)S(1)} fusion(f32[16,4,512]{2,1,0:T(4,128)S(1)} %get-tuple-element.192, s32[]{:T(128)S(6)} %copy.59, f32[4,512]{1,0:T(4,128)S(1)} %get-tuple-element.201, f32[512]{0:T(512)S(1)} %get-tuple-element.181, f32[512]{0:T(512)S(1)} %get-tuple-element.182, f32[512]{0:T(512)S(1)} %get-tuple-element.183, ...), kind=kOutput, calls=%fused_computation.2.clone.1 | convolution fusion | flops 14942208 | bytes 26628 | tf_op jit(solution)/shard_map/while/body/eval_jaxpr/dot_general | solution.py:30
  22.0 1.4 %fusion.59 = f32[16,4,512]{2,1,0:T(4,128)S(1)} fusion(f32[16,4,512]{2,1,0:T(4,128)S(1)} %get-tuple-element.192, s32[]{:T(128)S(6)} %copy.59, f32[4,512]{1,0:T(4,128)S(1)} %get-tuple-element.201, f32[512]{0:T(512)S(1)} %get-tuple-element.181, f32[512]{0:T(512)S(1)} %get-tuple-element.182, f32[512]{0:T(512)S(1)} %get-tuple-element.183, ...), kind=kOutput, calls=%fused_computation.2.clone.1 | convolution fusion | flops 14942208 | bytes 26628 | tf_op jit(solution)/shard_map/while/body/eval_jaxpr/dot_general | solution.py:30
  23.4 1.4 %fusion.59 = f32[16,4,512]{2,1,0:T(4,128)S(1)} fusion(f32[16,4,512]{2,1,0:T(4,128)S(1)} %get-tuple-element.192, s32[]{:T(128)S(6)} %copy.59, f32[4,512]{1,0:T(4,128)S(1)} %get-tuple-element.201, f32[512]{0:T(512)S(1)} %get-tuple-element.181, f32[512]{0:T(512)S(1)} %get-tuple-element.182, f32[512]{0:T(512)S(1)} %get-tuple-element.183, ...), kind=kOutput, calls=%fused_computation.2.clone.1 | convolution fusion | flops 14942208 | bytes 26628 | tf_op jit(solution)/shard_map/while/body/eval_jaxpr/dot_general | solution.py:30
  24.9 1.4 %fusion.59 = f32[16,4,512]{2,1,0:T(4,128)S(1)} fusion(f32[16,4,512]{2,1,0:T(4,128)S(1)} %get-tuple-element.192, s32[]{:T(128)S(6)} %copy.59, f32[4,512]{1,0:T(4,128)S(1)} %get-tuple-element.201, f32[512]{0:T(512)S(1)} %get-tuple-element.181, f32[512]{0:T(512)S(1)} %get-tuple-element.182, f32[512]{0:T(512)S(1)} %get-tuple-element.183, ...), kind=kOutput, calls=%fused_computation.2.clone.1 | convolution fusion | flops 14942208 | bytes 26628 | tf_op jit(solution)/shard_map/while/body/eval_jaxpr/dot_general | solution.py:30
  26.3 1.4 %fusion.59 = f32[16,4,512]{2,1,0:T(4,128)S(1)} fusion(f32[16,4,512]{2,1,0:T(4,128)S(1)} %get-tuple-element.192, s32[]{:T(128)S(6)} %copy.59, f32[4,512]{1,0:T(4,128)S(1)} %get-tuple-element.201, f32[512]{0:T(512)S(1)} %get-tuple-element.181, f32[512]{0:T(512)S(1)} %get-tuple-element.182, f32[512]{0:T(512)S(1)} %get-tuple-element.183, ...), kind=kOutput, calls=%fused_computation.2.clone.1 | convolution fusion | flops 14942208 | bytes 26628 | tf_op jit(solution)/shard_map/while/body/eval_jaxpr/dot_general | solution.py:30
  27.7 1.4 %fusion.59 = f32[16,4,512]{2,1,0:T(4,128)S(1)} fusion(f32[16,4,512]{2,1,0:T(4,128)S(1)} %get-tuple-element.192, s32[]{:T(128)S(6)} %copy.59, f32[4,512]{1,0:T(4,128)S(1)} %get-tuple-element.201, f32[512]{0:T(512)S(1)} %get-tuple-element.181, f32[512]{0:T(512)S(1)} %get-tuple-element.182, f32[512]{0:T(512)S(1)} %get-tuple-element.183, ...), kind=kOutput, calls=%fused_computation.2.clone.1 | convolution fusion | flops 14942208 | bytes 26628 | tf_op jit(solution)/shard_map/while/body/eval_jaxpr/dot_general | solution.py:30
  29.2 1.4 %fusion.59 = f32[16,4,512]{2,1,0:T(4,128)S(1)} fusion(f32[16,4,512]{2,1,0:T(4,128)S(1)} %get-tuple-element.192, s32[]{:T(128)S(6)} %copy.59, f32[4,512]{1,0:T(4,128)S(1)} %get-tuple-element.201, f32[512]{0:T(512)S(1)} %get-tuple-element.181, f32[512]{0:T(512)S(1)} %get-tuple-element.182, f32[512]{0:T(512)S(1)} %get-tuple-element.183, ...), kind=kOutput, calls=%fused_computation.2.clone.1 | convolution fusion | flops 14942208 | bytes 26628 | tf_op jit(solution)/shard_map/while/body/eval_jaxpr/dot_general | solution.py:30
  30.5 0.4 multiply_reduce_fusion.1
  31.0 0.1 reshape.294
  31.2 0.1 reshape.295
  31.3 0.7 copy-done
  32.1 0.7 copy-done.1
  32.9 0.1 stack.65
  33.1 0.1 stack.66
  33.3 0.1 stack.67
  33.5 0.1 reshape.296
  33.6 0.1 stack.68
  33.8 0.1 stack.69
  34.0 0.1 stack.70
  34.2 0.1 stack.71
  34.4 0.1 stack.72
  34.5 0.1 stack.73
  34.7 0.1 stack.74
  34.9 0.1 stack.75
  36.2 0.7 copy-done.6
  36.8 0.1 multiply_reduce_fusion
  36.9 0.6 copy-done.7
  37.5 0.3 fusion.39
  37.9 37.9 %psum.7 = f32[20,64]{0,1:T(8,128)S(1)} all-reduce(f32[20,64]{0,1:T(8,128)S(1)} %fusion.39), channel_id=1, replica_groups=mesh['sky'=4,'tm'=8] {'tm'}, use_global_device_ids=true, to_apply=%region_3.4 | all-reduce | flops 1280 | bytes 10240 | tf_op jit(solution)/shard_map/psum | solution.py:137
  75.8 0.7 copy-done.5
  76.5 0.1 copy.54
  76.8 0.1 subtract_divide_fusion.7
  76.9 0.1 subtract_divide_fusion.4
  77.1 0.1 subtract_divide_fusion
  77.3 0.7 copy.50
  (117 shorter events, 3.2 us)
Async XLA Ops:
  0.0 0.8 copy-start.3
  0.8 0.7 copy-start.4
  31.3 0.8 copy-start
  31.3 0.8 %copy-start.2 = (f32[8192]{0:T(1024)S(1)}, f32[8192]{0:T(1024)}, u32[]{:S(2)}) copy-start(f32[8192]{0:T(1024)} %param.14) | copy-start | bytes 98308
  32.1 0.8 copy-start.1
  36.1 0.7 copy-start.6
  36.8 0.7 copy-start.7
  75.8 0.7 copy-start.5
where the time goes:
time: 78.4 us; the launch traced here: 77.9 us
  blocking collectives  44.1 us (56%)
  matrix products  22.3 us (28%)
  local copies, waits for them, and re-layouts  9.75 us (12%)
  other arithmetic  1.07 us (1%)
    psum x1, blocking collectives, on_device(): total = lax.psum(partial_value, 'tm')  37.9 us
    dot_general x16, matrix products, one_block(): lax.dot_general(table, spread, (((1,), (1,)), ((), ())), precision=lax.Pr...  22 us
    all_gather x1, blocking collectives, on_device(): group = lax.all_gather(attitude, 'sky', axis=2, tiled=True)  6.15 us
    unnamed x40, local copies, waits for them, and re-layouts  4.73 us
    another operation x35, local copies, waits for them, and re-layouts, block_sums(): stacked = jnp.stack(rows)  2.6 us

commit v1 on v0

--- a/solution.py
+++ b/solution.py
@@ -134,7 +134,7 @@
     owned = prior.shape[1]
     sector_sources = owned * lax.axis_size("tm")
     partial_value = source_sums(sums, block_source, sector_sources)
-    total = lax.psum(partial_value, "tm")
+    total = jnp.sum(lax.all_gather(partial_value, "tm"), axis=0)
     normal = lax.dynamic_slice_in_dim(total, lax.axis_index("tm") * owned, owned, 1)
     return solve_normals(normal, prior)
 

time: 78.4 us -> 71.2 us (0.908)
  blocking collectives: 44.1 us -> 37.5 us
    psum x1 -> x0, blocking collectives: 37.9 us -> none  [on_device(): total = lax.psum(partial_value, 'tm')]
    all_gather x0 -> x1, blocking collectives: none -> 31.4 us  [on_device(): total = jnp.sum(lax.all_gather(partial_value, 'tm'), axis=0)]
    unnamed x40 -> x35, local copies, waits for them, and re-layouts: 4.73 us -> 4.32 us
where the time goes in v1:
time: 71.2 us; the launch traced here: 70.8 us
  blocking collectives  37.5 us (53%)
  matrix products  22.2 us (31%)
  local copies, waits for them, and re-layouts  9.2 us (13%)
  other arithmetic  1.11 us (2%)
    all_gather x1, blocking collectives, on_device(): total = jnp.sum(lax.all_gather(partial_value, 'tm'), axis=0)  31.4 us
    dot_general x16, matrix products, one_block(): lax.dot_general(table, spread, (((1,), (1,)), ((), ())), precision=lax.Pr...  22 us
    all_gather x1, blocking collectives, on_device(): group = lax.all_gather(attitude, 'sky', axis=2, tiled=True)  6.15 us
    unnamed x35, local copies, waits for them, and re-layouts  4.32 us
    another operation x35, local copies, waits for them, and re-layouts, block_sums(): stacked = jnp.stack(rows)  2.6 us

profile of v1, /device:TPU:0, one launch (start us, length us, event | category | flops | bytes accessed | tf_op | source)
XLA Modules:
  0.0 70.8 jit_solution(6305110734064752692)
XLA Ops:
  0.0 0.8 %reshape.292 = s32[16,512]{1,0:T(8,128)S(1)} reshape(s32[8192]{0:T(1024)} %param.16) | data formatting | bytes 65536 | tf_op jit(solution)/shard_map/reshape | solution.py:14
  0.8 0.7 copy-done.4
  1.5 6.2 %all_gather.9 = f32[4,1,512]{2,0,1:T(4,128)S(1)} all-gather(f32[4,1,128]{2,0,1:T(4,128)S(1)} %bitcast.35), channel_id=1, replica_groups=mesh['sky'=4,'tm'=8] {'sky'}, dimensions={2}, use_global_device_ids=true | all-gather | bytes 10240 | tf_op jit(solution)/shard_map/all_gather | solution.py:129
  7.6 22.9 %while.3 = (s32[]{:T(128)}, f32[16,4,512]{2,1,0:T(4,128)S(1)}, s32[16,512]{1,0:T(8,128)S(1)}, f32[16,512]{1,0:T(8,128)S(1)}, f32[4,512]{1,0:T(4,128)S(1)}, /*index=5*/s32[]{:T(128)}) while((s32[]{:T(128)}, f32[16,4,512]{2,1,0:T(4,128)S(1)}, s32[16,512]{1,0:T(8,128)S(1)}, f32[16,512]{1,0:T(8,128)S(1)}, f32[4,512]{1,0:T(4,128)S(1)}, ...), condition=%wide.region_1.2_spmd.clone, body=%wide.region_0.1_spmd.clone.sunk | while | flops 14951938 | bytes 45145 | solution.py:38
  7.6 1.4 %fusion.93 = f32[16,4,512]{2,1,0:T(4,128)S(1)} fusion(f32[16,4,512]{2,1,0:T(4,128)S(1)} %get-tuple-element.187, s32[]{:T(128)S(6)} %copy.36, f32[4,512]{1,0:T(4,128)S(1)} %get-tuple-element.196, f32[512]{0:T(512)S(1)} %get-tuple-element.176, f32[512]{0:T(512)S(1)} %get-tuple-element.177, f32[512]{0:T(512)S(1)} %get-tuple-element.178, ...), kind=kOutput, calls=%fused_computation.2.clone.1 | convolution fusion | flops 14942208 | bytes 26628 | tf_op jit(solution)/shard_map/while/body/eval_jaxpr/dot_general | solution.py:30
  9.1 1.4 %fusion.93 = f32[16,4,512]{2,1,0:T(4,128)S(1)} fusion(f32[16,4,512]{2,1,0:T(4,128)S(1)} %get-tuple-element.187, s32[]{:T(128)S(6)} %copy.36, f32[4,512]{1,0:T(4,128)S(1)} %get-tuple-element.196, f32[512]{0:T(512)S(1)} %get-tuple-element.176, f32[512]{0:T(512)S(1)} %get-tuple-element.177, f32[512]{0:T(512)S(1)} %get-tuple-element.178, ...), kind=kOutput, calls=%fused_computation.2.clone.1 | convolution fusion | flops 14942208 | bytes 26628 | tf_op jit(solution)/shard_map/while/body/eval_jaxpr/dot_general | solution.py:30
  10.5 1.4 %fusion.93 = f32[16,4,512]{2,1,0:T(4,128)S(1)} fusion(f32[16,4,512]{2,1,0:T(4,128)S(1)} %get-tuple-element.187, s32[]{:T(128)S(6)} %copy.36, f32[4,512]{1,0:T(4,128)S(1)} %get-tuple-element.196, f32[512]{0:T(512)S(1)} %get-tuple-element.176, f32[512]{0:T(512)S(1)} %get-tuple-element.177, f32[512]{0:T(512)S(1)} %get-tuple-element.178, ...), kind=kOutput, calls=%fused_computation.2.clone.1 | convolution fusion | flops 14942208 | bytes 26628 | tf_op jit(solution)/shard_map/while/body/eval_jaxpr/dot_general | solution.py:30
  12.0 1.4 %fusion.93 = f32[16,4,512]{2,1,0:T(4,128)S(1)} fusion(f32[16,4,512]{2,1,0:T(4,128)S(1)} %get-tuple-element.187, s32[]{:T(128)S(6)} %copy.36, f32[4,512]{1,0:T(4,128)S(1)} %get-tuple-element.196, f32[512]{0:T(512)S(1)} %get-tuple-element.176, f32[512]{0:T(512)S(1)} %get-tuple-element.177, f32[512]{0:T(512)S(1)} %get-tuple-element.178, ...), kind=kOutput, calls=%fused_computation.2.clone.1 | convolution fusion | flops 14942208 | bytes 26628 | tf_op jit(solution)/shard_map/while/body/eval_jaxpr/dot_general | solution.py:30
  13.4 1.4 %fusion.93 = f32[16,4,512]{2,1,0:T(4,128)S(1)} fusion(f32[16,4,512]{2,1,0:T(4,128)S(1)} %get-tuple-element.187, s32[]{:T(128)S(6)} %copy.36, f32[4,512]{1,0:T(4,128)S(1)} %get-tuple-element.196, f32[512]{0:T(512)S(1)} %get-tuple-element.176, f32[512]{0:T(512)S(1)} %get-tuple-element.177, f32[512]{0:T(512)S(1)} %get-tuple-element.178, ...), kind=kOutput, calls=%fused_computation.2.clone.1 | convolution fusion | flops 14942208 | bytes 26628 | tf_op jit(solution)/shard_map/while/body/eval_jaxpr/dot_general | solution.py:30
  14.8 1.4 %fusion.93 = f32[16,4,512]{2,1,0:T(4,128)S(1)} fusion(f32[16,4,512]{2,1,0:T(4,128)S(1)} %get-tuple-element.187, s32[]{:T(128)S(6)} %copy.36, f32[4,512]{1,0:T(4,128)S(1)} %get-tuple-element.196, f32[512]{0:T(512)S(1)} %get-tuple-element.176, f32[512]{0:T(512)S(1)} %get-tuple-element.177, f32[512]{0:T(512)S(1)} %get-tuple-element.178, ...), kind=kOutput, calls=%fused_computation.2.clone.1 | convolution fusion | flops 14942208 | bytes 26628 | tf_op jit(solution)/shard_map/while/body/eval_jaxpr/dot_general | solution.py:30
  16.3 1.4 %fusion.93 = f32[16,4,512]{2,1,0:T(4,128)S(1)} fusion(f32[16,4,512]{2,1,0:T(4,128)S(1)} %get-tuple-element.187, s32[]{:T(128)S(6)} %copy.36, f32[4,512]{1,0:T(4,128)S(1)} %get-tuple-element.196, f32[512]{0:T(512)S(1)} %get-tuple-element.176, f32[512]{0:T(512)S(1)} %get-tuple-element.177, f32[512]{0:T(512)S(1)} %get-tuple-element.178, ...), kind=kOutput, calls=%fused_computation.2.clone.1 | convolution fusion | flops 14942208 | bytes 26628 | tf_op jit(solution)/shard_map/while/body/eval_jaxpr/dot_general | solution.py:30
  17.7 1.4 %fusion.93 = f32[16,4,512]{2,1,0:T(4,128)S(1)} fusion(f32[16,4,512]{2,1,0:T(4,128)S(1)} %get-tuple-element.187, s32[]{:T(128)S(6)} %copy.36, f32[4,512]{1,0:T(4,128)S(1)} %get-tuple-element.196, f32[512]{0:T(512)S(1)} %get-tuple-element.176, f32[512]{0:T(512)S(1)} %get-tuple-element.177, f32[512]{0:T(512)S(1)} %get-tuple-element.178, ...), kind=kOutput, calls=%fused_computation.2.clone.1 | convolution fusion | flops 14942208 | bytes 26628 | tf_op jit(solution)/shard_map/while/body/eval_jaxpr/dot_general | solution.py:30
  19.1 1.4 %fusion.93 = f32[16,4,512]{2,1,0:T(4,128)S(1)} fusion(f32[16,4,512]{2,1,0:T(4,128)S(1)} %get-tuple-element.187, s32[]{:T(128)S(6)} %copy.36, f32[4,512]{1,0:T(4,128)S(1)} %get-tuple-element.196, f32[512]{0:T(512)S(1)} %get-tuple-element.176, f32[512]{0:T(512)S(1)} %get-tuple-element.177, f32[512]{0:T(512)S(1)} %get-tuple-element.178, ...), kind=kOutput, calls=%fused_computation.2.clone.1 | convolution fusion | flops 14942208 | bytes 26628 | tf_op jit(solution)/shard_map/while/body/eval_jaxpr/dot_general | solution.py:30
  20.6 1.4 %fusion.93 = f32[16,4,512]{2,1,0:T(4,128)S(1)} fusion(f32[16,4,512]{2,1,0:T(4,128)S(1)} %get-tuple-element.187, s32[]{:T(128)S(6)} %copy.36, f32[4,512]{1,0:T(4,128)S(1)} %get-tuple-element.196, f32[512]{0:T(512)S(1)} %get-tuple-element.176, f32[512]{0:T(512)S(1)} %get-tuple-element.177, f32[512]{0:T(512)S(1)} %get-tuple-element.178, ...), kind=kOutput, calls=%fused_computation.2.clone.1 | convolution fusion | flops 14942208 | bytes 26628 | tf_op jit(solution)/shard_map/while/body/eval_jaxpr/dot_general | solution.py:30
  22.0 1.4 %fusion.93 = f32[16,4,512]{2,1,0:T(4,128)S(1)} fusion(f32[16,4,512]{2,1,0:T(4,128)S(1)} %get-tuple-element.187, s32[]{:T(128)S(6)} %copy.36, f32[4,512]{1,0:T(4,128)S(1)} %get-tuple-element.196, f32[512]{0:T(512)S(1)} %get-tuple-element.176, f32[512]{0:T(512)S(1)} %get-tuple-element.177, f32[512]{0:T(512)S(1)} %get-tuple-element.178, ...), kind=kOutput, calls=%fused_computation.2.clone.1 | convolution fusion | flops 14942208 | bytes 26628 | tf_op jit(solution)/shard_map/while/body/eval_jaxpr/dot_general | solution.py:30
  23.4 1.4 %fusion.93 = f32[16,4,512]{2,1,0:T(4,128)S(1)} fusion(f32[16,4,512]{2,1,0:T(4,128)S(1)} %get-tuple-element.187, s32[]{:T(128)S(6)} %copy.36, f32[4,512]{1,0:T(4,128)S(1)} %get-tuple-element.196, f32[512]{0:T(512)S(1)} %get-tuple-element.176, f32[512]{0:T(512)S(1)} %get-tuple-element.177, f32[512]{0:T(512)S(1)} %get-tuple-element.178, ...), kind=kOutput, calls=%fused_computation.2.clone.1 | convolution fusion | flops 14942208 | bytes 26628 | tf_op jit(solution)/shard_map/while/body/eval_jaxpr/dot_general | solution.py:30
  24.9 1.4 %fusion.93 = f32[16,4,512]{2,1,0:T(4,128)S(1)} fusion(f32[16,4,512]{2,1,0:T(4,128)S(1)} %get-tuple-element.187, s32[]{:T(128)S(6)} %copy.36, f32[4,512]{1,0:T(4,128)S(1)} %get-tuple-element.196, f32[512]{0:T(512)S(1)} %get-tuple-element.176, f32[512]{0:T(512)S(1)} %get-tuple-element.177, f32[512]{0:T(512)S(1)} %get-tuple-element.178, ...), kind=kOutput, calls=%fused_computation.2.clone.1 | convolution fusion | flops 14942208 | bytes 26628 | tf_op jit(solution)/shard_map/while/body/eval_jaxpr/dot_general | solution.py:30
  26.3 1.4 %fusion.93 = f32[16,4,512]{2,1,0:T(4,128)S(1)} fusion(f32[16,4,512]{2,1,0:T(4,128)S(1)} %get-tuple-element.187, s32[]{:T(128)S(6)} %copy.36, f32[4,512]{1,0:T(4,128)S(1)} %get-tuple-element.196, f32[512]{0:T(512)S(1)} %get-tuple-element.176, f32[512]{0:T(512)S(1)} %get-tuple-element.177, f32[512]{0:T(512)S(1)} %get-tuple-element.178, ...), kind=kOutput, calls=%fused_computation.2.clone.1 | convolution fusion | flops 14942208 | bytes 26628 | tf_op jit(solution)/shard_map/while/body/eval_jaxpr/dot_general | solution.py:30
  27.7 1.4 %fusion.93 = f32[16,4,512]{2,1,0:T(4,128)S(1)} fusion(f32[16,4,512]{2,1,0:T(4,128)S(1)} %get-tuple-element.187, s32[]{:T(128)S(6)} %copy.36, f32[4,512]{1,0:T(4,128)S(1)} %get-tuple-element.196, f32[512]{0:T(512)S(1)} %get-tuple-element.176, f32[512]{0:T(512)S(1)} %get-tuple-element.177, f32[512]{0:T(512)S(1)} %get-tuple-element.178, ...), kind=kOutput, calls=%fused_computation.2.clone.1 | convolution fusion | flops 14942208 | bytes 26628 | tf_op jit(solution)/shard_map/while/body/eval_jaxpr/dot_general | solution.py:30
  29.2 1.4 %fusion.93 = f32[16,4,512]{2,1,0:T(4,128)S(1)} fusion(f32[16,4,512]{2,1,0:T(4,128)S(1)} %get-tuple-element.187, s32[]{:T(128)S(6)} %copy.36, f32[4,512]{1,0:T(4,128)S(1)} %get-tuple-element.196, f32[512]{0:T(512)S(1)} %get-tuple-element.176, f32[512]{0:T(512)S(1)} %get-tuple-element.177, f32[512]{0:T(512)S(1)} %get-tuple-element.178, ...), kind=kOutput, calls=%fused_computation.2.clone.1 | convolution fusion | flops 14942208 | bytes 26628 | tf_op jit(solution)/shard_map/while/body/eval_jaxpr/dot_general | solution.py:30
  30.5 0.4 multiply_reduce_fusion.1
  31.0 0.1 reshape.294
  31.2 0.1 reshape.295
  31.3 0.7 %copy-done = f32[8192]{0:T(1024)S(1)} copy-done((f32[8192]{0:T(1024)S(1)}, f32[8192]{0:T(1024)}, u32[]{:S(2)}) %copy-start) | copy-done | bytes 32792
  32.1 0.7 %copy-done.1 = f32[8192]{0:T(1024)S(1)} copy-done((f32[8192]{0:T(1024)S(1)}, f32[8192]{0:T(1024)}, u32[]{:S(2)}) %copy-start.1) | copy-done | bytes 32792
  32.9 0.1 stack.65
  33.1 0.1 stack.66
  33.3 0.1 stack.67
  33.5 0.1 reshape.296
  33.6 0.1 stack.68
  33.8 0.1 stack.69
  34.0 0.1 stack.70
  34.2 0.1 stack.71
  34.4 0.1 stack.72
  34.5 0.1 stack.73
  34.7 0.1 stack.74
  34.9 0.1 stack.75
  35.1 0.1 stack.76
  36.2 0.7 copy-done.6
  36.8 0.1 multiply_reduce_fusion
  36.9 0.6 copy-done.7
  37.5 0.2 convolution_bitcast_fusion.1
  37.8 31.4 %all-gather.1 = f32[8,20,64]{2,1,0:T(8,128)S(1)} all-gather(f32[1,20,64]{2,1,0:T(8,128)S(1)} %convolution_bitcast_fusion.1), channel_id=2, replica_groups=mesh['sky'=4,'tm'=8] {'tm'}, dimensions={0}, use_global_device_ids=true | all-gather | bytes 46080 | tf_op jit(solution)/shard_map/all_gather | solution.py:137
  69.2 0.7 copy-done.5
  69.9 0.1 fusion.66
  70.0 0.1 fusion.67
  70.1 0.1 subtract_divide_fusion
  70.2 0.6 stack.83
  (110 shorter events, 2.8 us)
Async XLA Ops:
  0.0 0.8 %copy-start.3 = (f32[8192]{0:T(1024)S(1)}, f32[8192]{0:T(1024)}, u32[]{:S(2)}) copy-start(f32[8192]{0:T(1024)} %param.15) | copy-start | bytes 98308
  0.8 0.7 copy-start.4
  31.3 0.8 %copy-start = (f32[8192]{0:T(1024)S(1)}, f32[8192]{0:T(1024)}, u32[]{:S(2)}) copy-start(f32[8192]{0:T(1024)} %param.12) | copy-start | bytes 98308
  31.3 0.8 %copy-start.2 = (f32[8192]{0:T(1024)S(1)}, f32[8192]{0:T(1024)}, u32[]{:S(2)}) copy-start(f32[8192]{0:T(1024)} %param.14) | copy-start | bytes 98308
  32.1 0.8 %copy-start.1 = (f32[8192]{0:T(1024)S(1)}, f32[8192]{0:T(1024)}, u32[]{:S(2)}) copy-start(f32[8192]{0:T(1024)} %param.13) | copy-start | bytes 98308
  36.1 0.7 copy-start.6
  36.8 0.7 copy-start.7
  69.2 0.7 copy-start.5
